TPU v7x, 32 devices: a whole 2x2x4 slice. The times are simulated.
32 devices in a mesh: fsdp: 4 (over y, x), seq: 8 (over z, core).
Axes of the slice: x: 2, y: 2, z: 4, core: 2. Of those that a mesh axis runs over, the one named last changes fastest.
Arguments:
- images: bfloat16 [32, 1024, 1152], P('fsdp', 'seq'), may hold values from -8 to 8
- lengths: int32 [32], P('fsdp'), may hold values from 256 to 1024
- ln1_gain: bfloat16 [1152], P('fsdp'), may hold values from 0.099609375 to 1.8984375
- ln1_bias: bfloat16 [1152], P('fsdp'), may hold values from -3 to 3
- w_qkv: bfloat16 [1152, 3456], P('fsdp'), may hold values from -1 to 1
- qv_bias: bfloat16 [2, 1152], P(None, 'fsdp'), may hold values from -3 to 3
- w_out: bfloat16 [1152, 1152], P('fsdp'), may hold values from -0.75 to 0.75
- out_bias: bfloat16 [1152], P('fsdp'), may hold values from -3 to 3
- ln2_gain: bfloat16 [1152], P('fsdp'), may hold values from 0.099609375 to 1.8984375
- ln2_bias: bfloat16 [1152], P('fsdp'), may hold values from -3 to 3
- w_up: bfloat16 [1152, 4304], P('fsdp'), may hold values from -0.1875 to 0.1875
- up_bias: bfloat16 [4304], P('fsdp'), may hold values from -3 to 3
- w_down: bfloat16 [4304, 1152], P(None, 'fsdp'), may hold values from -0.09375 to 0.09375
- down_bias: bfloat16 [1152], P('fsdp'), may hold values from -3 to 3
- cotangent: bfloat16 [32, 1024, 1152], P('fsdp', 'seq'), may hold values from -6 to 6
Outputs:
- layer_out: bfloat16 [32, 1024, 1152], P('fsdp', 'seq')
- grad_images: bfloat16 [32, 1024, 1152], P('fsdp', 'seq')
- grad_ln1_gain: float32 [1152], P('fsdp')
- grad_ln1_bias: float32 [1152], P('fsdp')
- grad_w_qkv: float32 [1152, 3456], P('fsdp')
- grad_qv_bias: float32 [2, 1152], P(None, 'fsdp')
- grad_w_out: float32 [1152, 1152], P('fsdp')
- grad_out_bias: float32 [1152], P('fsdp')
- grad_ln2_gain: float32 [1152], P('fsdp')
- grad_ln2_bias: float32 [1152], P('fsdp')
- grad_w_up: float32 [1152, 4304], P('fsdp')
- grad_up_bias: float32 [4304], P('fsdp')
- grad_w_down: float32 [4304, 1152], P(None, 'fsdp')
- grad_down_bias: float32 [1152], P('fsdp')
All inputs are finite; a program needn't handle non-finite values.
Results may differ from a plain program's by a relative error of at most 0.017.
Values may be sent and summed in bfloat16 or wider, within the bound.
A program may use at most 256 MiB of HBM per device.

v0:
```python
import jax
import jax.numpy as jnp
from jax import lax
from jax.sharding import PartitionSpec as P

H = 16
HD = 72
epsilon = 1e-06
wide_block = 1024


def for_sending(shard):

    def short(part):
        return part.astype(jnp.bfloat16) if part.dtype == jnp.float32 else part

    return jax.tree.map(short, shard)


def normalize(field, gain_vec, bias_vec):
    center_mean = jnp.mean(field, -1, keepdims=True)
    centered = field - center_mean
    variance = jnp.mean(centered * centered, -1, keepdims=True)
    return centered * lax.rsqrt(variance + epsilon) * gain_vec + bias_vec


def gelu_tanh(field):
    return jax.nn.gelu(field, approximate=True)


def attend_item(queries, keys_all, values, length_one):
    length_all = keys_all.shape[1]
    block_rows = min(wide_block, length_all)
    visible = (jnp.arange(length_all) < length_one)[None, :]
    pieces = []
    log_sums = []
    for offset in range(0, length_all, block_rows):
        scores = jnp.einsum(
            "dq,dk->qk",
            queries[:, offset : offset + block_rows],
            keys_all,
            preferred_element_type=jnp.float32,
        )
        scores = jnp.where(visible, scores, -1e30)
        row_max = jnp.max(scores, -1, keepdims=True)
        exponents = jnp.exp(scores - row_max)
        denominator = jnp.sum(exponents, -1, keepdims=True)
        softmax_low = (exponents / denominator).astype(jnp.bfloat16)
        pieces.append(
            jnp.einsum("qk,dk->dq", softmax_low, values, preferred_element_type=jnp.float32)
        )
        log_sums.append(row_max[:, 0] + jnp.log(denominator[:, 0]))
    return (jnp.concatenate(pieces, 1).astype(jnp.bfloat16), jnp.concatenate(log_sums, 0))


def attend_back(queries, keys_all, values, length_one, log_sum, grad_mixed):
    length_all = keys_all.shape[1]
    block_rows = min(wide_block, length_all)
    visible = (jnp.arange(length_all) < length_one)[None, :]
    grad_keys = jnp.zeros(keys_all.shape, jnp.float32)
    grad_values = jnp.zeros(values.shape, jnp.float32)
    grad_pieces = []
    for offset in range(0, length_all, block_rows):
        query_rows = queries[:, offset : offset + block_rows]
        grad_rows = grad_mixed[:, offset : offset + block_rows]
        scores = jnp.einsum("dq,dk->qk", query_rows, keys_all, preferred_element_type=jnp.float32)
        scores = jnp.where(visible, scores, -1e30)
        softmax_out = jnp.exp(scores - log_sum[offset : offset + block_rows, None])
        grad_soft = jnp.einsum("dq,dk->qk", grad_rows, values, preferred_element_type=jnp.float32)
        row_dot = jnp.sum(softmax_out * grad_soft, -1, keepdims=True)
        grad_scores = (softmax_out * (grad_soft - row_dot)).astype(jnp.bfloat16)
        grad_pieces.append(
            jnp.einsum("qk,dk->dq", grad_scores, keys_all, preferred_element_type=jnp.float32)
        )
        grad_keys = grad_keys + jnp.einsum(
            "qk,dq->dk", grad_scores, query_rows, preferred_element_type=jnp.float32
        )
        grad_values = grad_values + jnp.einsum(
            "qk,dq->dk",
            softmax_out.astype(jnp.bfloat16),
            grad_rows,
            preferred_element_type=jnp.float32,
        )
    return (
        jnp.concatenate(grad_pieces, 1).astype(jnp.bfloat16),
        grad_keys.astype(jnp.bfloat16),
        grad_values.astype(jnp.bfloat16),
    )


def on_device(
    images,
    lengths,
    ln1_gain,
    ln1_bias,
    w_qkv,
    qv_bias,
    w_out,
    out_bias,
    ln2_gain,
    ln2_bias,
    w_up,
    up_bias,
    w_down,
    down_bias,
    cotangent,
):
    image_count, token_count, width_all = images.shape
    head_scale = HD ** (-0.5)
    gain_first, bias_first, qkv_full, qv_full, out_full, outb_full = (
        lax.all_gather(ln1_gain, "fsdp", axis=0, tiled=True),
        lax.all_gather(ln1_bias, "fsdp", axis=0, tiled=True),
        lax.all_gather(w_qkv, "fsdp", axis=0, tiled=True),
        lax.all_gather(qv_bias, "fsdp", axis=1, tiled=True),
        lax.all_gather(w_out, "fsdp", axis=0, tiled=True),
        lax.all_gather(out_bias, "fsdp", axis=0, tiled=True),
    )
    inputs_all = images.astype(jnp.float32)
    normed_first, norm_first_back = jax.vjp(
        normalize, inputs_all, gain_first.astype(jnp.float32), bias_first.astype(jnp.float32)
    )
    normed_attn = normed_first.astype(jnp.bfloat16)
    qkv_split = qkv_full.reshape(width_all, 3, H, HD)
    projected = jnp.einsum(
        "itd,dahe->ahiet", normed_attn, qkv_split, preferred_element_type=jnp.float32
    )
    shift_pair = qv_full.astype(jnp.float32).reshape(2, H, HD)
    queries = (projected[0] + shift_pair[0][:, None, :, None]) * head_scale
    values = projected[2] + shift_pair[1][:, None, :, None]
    stacked = jnp.stack([queries, projected[1], values]).astype(jnp.bfloat16)
    head_view = lax.all_to_all(stacked, "seq", split_axis=1, concat_axis=4, tiled=True)
    local_heads = head_view.shape[1]
    item_count = local_heads * image_count
    query_items = head_view[0].reshape(item_count, HD, -1)
    key_items = head_view[1].reshape(item_count, HD, -1)
    value_items = head_view[2].reshape(item_count, HD, -1)
    item_lengths = jnp.tile(lengths, local_heads)
    mixed_items, log_sums = lax.map(
        lambda packed: attend_item(*packed), (query_items, key_items, value_items, item_lengths)
    )
    mixed_tokens = lax.all_to_all(
        for_sending(mixed_items.reshape(local_heads, image_count, HD, -1)),
        "seq",
        split_axis=3,
        concat_axis=0,
        tiled=True,
    )
    out_split = out_full.reshape(H, HD, width_all)
    residual = (
        inputs_all
        + jnp.einsum("hiet,hed->itd", mixed_tokens, out_split, preferred_element_type=jnp.float32)
        + outb_full.astype(jnp.float32)
    )
    gain_second, bias_second, up_full, upb_full, down_full, downb_full = (
        lax.all_gather(ln2_gain, "fsdp", axis=0, tiled=True),
        lax.all_gather(ln2_bias, "fsdp", axis=0, tiled=True),
        lax.all_gather(w_up, "fsdp", axis=0, tiled=True),
        lax.all_gather(up_bias, "fsdp", axis=0, tiled=True),
        lax.all_gather(w_down, "fsdp", axis=1, tiled=True),
        lax.all_gather(down_bias, "fsdp", axis=0, tiled=True),
    )
    normed_second, norm_second_back = jax.vjp(
        normalize, residual, gain_second.astype(jnp.float32), bias_second.astype(jnp.float32)
    )
    normed_mlp = normed_second.astype(jnp.bfloat16)
    pre_act = jnp.einsum(
        "itd,df->itf", normed_mlp, up_full, preferred_element_type=jnp.float32
    ) + upb_full.astype(jnp.float32)
    activation, gelu_back = jax.vjp(gelu_tanh, pre_act)
    activation = activation.astype(jnp.bfloat16)
    output_all = (
        residual
        + jnp.einsum("itf,fd->itd", activation, down_full, preferred_element_type=jnp.float32)
        + downb_full.astype(jnp.float32)
    )
    layer_out = output_all.astype(jnp.bfloat16)
    qkv_back, out_back = (
        lax.all_gather(w_qkv, "fsdp", axis=0, tiled=True),
        lax.all_gather(w_out, "fsdp", axis=0, tiled=True),
    )
    up_back, down_back = (
        lax.all_gather(w_up, "fsdp", axis=0, tiled=True),
        lax.all_gather(w_down, "fsdp", axis=1, tiled=True),
    )
    grad_down = jnp.einsum("itf,itd->fd", activation, cotangent, preferred_element_type=jnp.float32)
    grad_downb = jnp.sum(cotangent, axis=(0, 1), dtype=jnp.float32)
    grad_act = jnp.einsum("itd,fd->itf", cotangent, down_back, preferred_element_type=jnp.float32)
    (grad_pre,) = gelu_back(grad_act)
    grad_pre = grad_pre.astype(jnp.bfloat16)
    grad_up = jnp.einsum("itd,itf->df", normed_mlp, grad_pre, preferred_element_type=jnp.float32)
    grad_upb = jnp.sum(grad_pre, axis=(0, 1), dtype=jnp.float32)
    grad_normed_mlp = jnp.einsum(
        "itf,df->itd", grad_pre, up_back, preferred_element_type=jnp.float32
    )
    grad_resid_norm, grad_gain_second, grad_bias_second = norm_second_back(grad_normed_mlp)
    grad_residual = cotangent.astype(jnp.float32) + grad_resid_norm
    grad_branch = grad_residual.astype(jnp.bfloat16)
    grad_outw = jnp.einsum(
        "hiet,itd->hed", mixed_tokens, grad_branch, preferred_element_type=jnp.float32
    ).reshape(width_all, width_all)
    grad_outb = jnp.sum(grad_branch, axis=(0, 1), dtype=jnp.float32)
    out_back_split = out_back.reshape(H, HD, width_all)
    grad_mixed = jnp.einsum(
        "itd,hed->hiet", grad_branch, out_back_split, preferred_element_type=jnp.float32
    ).astype(jnp.bfloat16)
    grad_head_view = lax.all_to_all(grad_mixed, "seq", split_axis=0, concat_axis=3, tiled=True)
    grad_items = grad_head_view.reshape(item_count, HD, -1)
    grad_q, grad_k, grad_v = lax.map(
        lambda packed: attend_back(*packed),
        (query_items, key_items, value_items, item_lengths, log_sums, grad_items),
    )
    grad_stack = jnp.stack([grad_q, grad_k, grad_v]).reshape(3, local_heads, image_count, HD, -1)
    grad_projected = lax.all_to_all(
        for_sending(grad_stack), "seq", split_axis=4, concat_axis=1, tiled=True
    ).astype(grad_stack.dtype)
    column_scales = jnp.array([head_scale, 1.0, 1.0], jnp.float32)
    grad_qkv = (
        jnp.einsum(
            "itd,ahiet->dahe", normed_attn, grad_projected, preferred_element_type=jnp.float32
        )
        * column_scales[None, :, None, None]
    ).reshape(width_all, 3 * width_all)
    shift_sums = jnp.sum(grad_projected, axis=(2, 4), dtype=jnp.float32)
    grad_qvb = jnp.stack([shift_sums[0] * head_scale, shift_sums[2]]).reshape(2, width_all)
    qkv_back_split = qkv_back.reshape(width_all, 3, H, HD)
    grad_normed_attn = head_scale * jnp.einsum(
        "hiet,dhe->itd", grad_projected[0], qkv_back_split[:, 0], preferred_element_type=jnp.float32
    )
    grad_normed_attn = grad_normed_attn + jnp.einsum(
        "ahiet,dahe->itd",
        grad_projected[1:],
        qkv_back_split[:, 1:],
        preferred_element_type=jnp.float32,
    )
    grad_input_norm, grad_gain_first, grad_bias_first = norm_first_back(grad_normed_attn)
    grad_images = (grad_residual + grad_input_norm).astype(jnp.bfloat16)
    (
        part_gone,
        part_bone,
        part_qkv,
        part_qvb,
        part_outw,
        part_outb,
        part_gtwo,
        part_btwo,
        part_up,
        part_upb,
        part_down,
        part_downb,
    ) = (
        lax.psum_scatter(
            grad_gain_first.astype(jnp.bfloat16), "fsdp", scatter_dimension=0, tiled=True
        ).astype(jnp.float32),
        lax.psum_scatter(
            grad_bias_first.astype(jnp.bfloat16), "fsdp", scatter_dimension=0, tiled=True
        ).astype(jnp.float32),
        lax.psum_scatter(
            grad_qkv.astype(jnp.bfloat16), "fsdp", scatter_dimension=0, tiled=True
        ).astype(jnp.float32),
        lax.psum_scatter(
            grad_qvb.astype(jnp.bfloat16), "fsdp", scatter_dimension=1, tiled=True
        ).astype(jnp.float32),
        lax.psum_scatter(
            grad_outw.astype(jnp.bfloat16), "fsdp", scatter_dimension=0, tiled=True
        ).astype(jnp.float32),
        lax.psum_scatter(
            grad_outb.astype(jnp.bfloat16), "fsdp", scatter_dimension=0, tiled=True
        ).astype(jnp.float32),
        lax.psum_scatter(
            grad_gain_second.astype(jnp.bfloat16), "fsdp", scatter_dimension=0, tiled=True
        ).astype(jnp.float32),
        lax.psum_scatter(
            grad_bias_second.astype(jnp.bfloat16), "fsdp", scatter_dimension=0, tiled=True
        ).astype(jnp.float32),
        lax.psum_scatter(
            grad_up.astype(jnp.bfloat16), "fsdp", scatter_dimension=0, tiled=True
        ).astype(jnp.float32),
        lax.psum_scatter(
            grad_upb.astype(jnp.bfloat16), "fsdp", scatter_dimension=0, tiled=True
        ).astype(jnp.float32),
        lax.psum_scatter(
            grad_down.astype(jnp.bfloat16), "fsdp", scatter_dimension=1, tiled=True
        ).astype(jnp.float32),
        lax.psum_scatter(
            grad_downb.astype(jnp.bfloat16), "fsdp", scatter_dimension=0, tiled=True
        ).astype(jnp.float32),
    )
    (
        final_gone,
        final_bone,
        final_qkv,
        final_qvb,
        final_outw,
        final_outb,
        final_gtwo,
        final_btwo,
        final_up,
        final_upb,
        final_down,
        final_downb,
    ) = (
        lax.psum(part_gone.astype(jnp.bfloat16), "seq").astype(jnp.float32),
        lax.psum(part_bone.astype(jnp.bfloat16), "seq").astype(jnp.float32),
        lax.psum(part_qkv.astype(jnp.bfloat16), "seq").astype(jnp.float32),
        lax.psum(part_qvb.astype(jnp.bfloat16), "seq").astype(jnp.float32),
        lax.psum(part_outw.astype(jnp.bfloat16), "seq").astype(jnp.float32),
        lax.psum(part_outb.astype(jnp.bfloat16), "seq").astype(jnp.float32),
        lax.psum(part_gtwo.astype(jnp.bfloat16), "seq").astype(jnp.float32),
        lax.psum(part_btwo.astype(jnp.bfloat16), "seq").astype(jnp.float32),
        lax.psum(part_up.astype(jnp.bfloat16), "seq").astype(jnp.float32),
        lax.psum(part_upb.astype(jnp.bfloat16), "seq").astype(jnp.float32),
        lax.psum(part_down.astype(jnp.bfloat16), "seq").astype(jnp.float32),
        lax.psum(part_downb.astype(jnp.bfloat16), "seq").astype(jnp.float32),
    )
    return (
        layer_out,
        grad_images,
        final_gone,
        final_bone,
        final_qkv,
        final_qvb,
        final_outw,
        final_outb,
        final_gtwo,
        final_btwo,
        final_up,
        final_upb,
        final_down,
        final_downb,
    )


def solution(mesh):
    placed = (
        P("fsdp", "seq", None),
        P("fsdp"),
        P("fsdp"),
        P("fsdp"),
        P("fsdp", None),
        P(None, "fsdp"),
        P("fsdp", None),
        P("fsdp"),
        P("fsdp"),
        P("fsdp"),
        P("fsdp", None),
        P("fsdp"),
        P(None, "fsdp"),
        P("fsdp"),
        P("fsdp", "seq", None),
    )
    return jax.shard_map(
        on_device,
        mesh=mesh,
        in_specs=placed,
        out_specs=(
            P("fsdp", "seq", None),
            P("fsdp", "seq", None),
            P("fsdp"),
            P("fsdp"),
            P("fsdp", None),
            P(None, "fsdp"),
            P("fsdp", None),
            P("fsdp"),
            P("fsdp"),
            P("fsdp"),
            P("fsdp", None),
            P("fsdp"),
            P(None, "fsdp"),
            P("fsdp"),
        ),
        check_vma=False,
    )
```

profile of v0, /device:TPU:0, one launch (start us, length us, event | category | flops | bytes accessed | tf_op | source)
XLA Modules:
  0.0 1667.9 jit_solution(1936642603031009704)
XLA Ops:
  13.0 18.5 %all-reduce.17 = (bf16[1152]{0:T(1024)(128)(2,1)S(1)}, bf16[1152]{0:T(1024)(128)(2,1)S(1)}, bf16[1152]{0:T(1024)(128)(2,1)S(1)}, bf16[1152]{0:T(1024)(128)(2,1)S...) all-reduce(bf16[1152]{0:T(1024)(128)(2,1)S(1)} %dynamic-update-slic, ...), channel_id=1, replica_groups=mesh['fsdp'=4,'seq'=8] {'fsdp'}, use_global_device_ids=true, to_apply=%add.1 | all-reduce | flops 10064 | bytes 40256
  33.3 7.5 all-gather
  41.1 55.8 %all-gather.6.cloned.1.call-done = bf16[1152,3456]{1,0:T(8,128)(2,1)} async-done(((bf16[288,3456]{1,0:T(8,128)(2,1)}), bf16[1152,3456]{1,0:T(8,128)(2,1)}) %all-gather.6.cloned.1.call-update) | async-done | bytes 7962640 | tf_op jit(solution)/shard_map/all_gather | solution.py:113
  96.9 11.5 copy.97
  108.5 12.5 convolution_bitcast_fusion.3
  123.5 4.8 copy.99
  128.3 5.0 all-to-all-start
  133.9 155.1 %all-to-all-done = bf16[3,16,8,72,128]{4,3,0,2,1:T(8,128)(2,1)} async-done(((bf16[3,16,8,72,128]{4,3,0,2,1:T(8,128)(2,1)}), bf16[3,16,8,72,128]{4,3,0,2,1:T(8,128)(2,1)}, u32[]{:S(2)}, u32[]{:S(2)}) %all-to-all-start) | async-done | bytes 7077920 | tf_op jit(solution)/shard_map/all_to_all | solution.py:131
  289.0 7.7 fusion.114
  299.6 5.0 reshape_squeeze.10
  304.6 4.6 copy.102
  309.2 4.9 reshape_squeeze.11
  314.1 4.6 copy.100
  318.7 4.9 reshape_squeeze.9
  325.3 180.0 %while.26 = (s32[]{:T(128)}, bf16[16,72,1024]{2,1,0:T(8,128)(2,1)}, f32[16,1024]{1,0:T(8,128)}, bf16[16,72,1024]{2,1,0:T(8,128)(2,1)}, s32[16]{0:T(128)S(1)}, /*...) while((s32[]{:T(128)}, bf16[16,72,1024]{2,1,0:T(8,128)(2,1)}, ...), condition=%wide.region_5.6_spmd, body=%wide.region_2.5_spmd.sunk | while | flops 311500800 | bytes 29997196 | solution.py:138
  505.4 6.3 copy.103
  511.7 4.5 all-to-all-start.1
  516.7 93.5 %all-to-all-done.1 = bf16[2,8,72,1024]{2,1,0,3:T(8,128)(2,1)} async-done(((bf16[2,8,72,1024]{2,1,0,3:T(8,128)(2,1)}), bf16[2,8,72,1024]{2,1,0,3:T(8,128)(2,1)}, u32[]{:S(2)}, u32[]{:S(2)}) %all-to-all-start.1) | async-done | bytes 2359328 | tf_op jit(solution)/shard_map/all_to_all | solution.py:141
  610.2 6.3 copy.105
  616.5 6.5 fusion.116
  625.9 24.8 %multiply_convert_fusion.1 = (bf16[8,128,4304]{1,2,0:T(8,128)(2,1)}, f32[8,128,4304]{1,2,0:T(8,128)}) fusion(f32[4304]{0:T(1024)S(1)} %convert_element_type.186, bf16[1152,4304]{1,0:T(8,128)(2,1)} %all-gather.10.cloned.1.call-done, f32[8,128,1152]{2,1,0:T(8,128)} %copy-done.5, f32[1152]{0:T(1024)S(1)} %convert_element_type.184, ...), kind=kOutput, calls=%fused_computation.72 | convolution fusion | flops 10204381184 | bytes 41113408 | tf_op jit(solution)/shard_map/itd,df->itf/dot_general | solution.py:166
  650.7 32.5 %fusion.117 = (bf16[4304]{0:T(1024)(128)(2,1)}, bf16[8,128,4304]{1,2,0:T(8,128)(2,1)}) fusion(f32[8,128,4304]{1,2,0:T(8,128)} %get-tuple-element.199, f32[4304]{0:T(1024)S(1)} %convert_element_type.186, bf16[8,128,1152]{2,1,0:T(8,128)(2,1)} %param.34, bf16[4304,1152]{0,1:T(8,128)(2,1)} %all-gather.12.cloned.1.call-done), kind=kOutput, calls=%fused_computation.155 | convolution fusion | flops 10251366400 | bytes 38745312 | tf_op jit(solution)/shard_map/itd,fd->itf/dot_general | solution.py:187
  683.2 20.6 %multiply_reduce_fusion.1 = (bf16[1152]{0:T(1024)(128)(2,1)}, f32[8,128]{1,0:T(8,128)S(1)}, bf16[1152]{0:T(1024)(128)(2,1)}, f32[8,128,1152]{2,1,0:T(8,128)}) fusion(f32[8,128,1152]{2,1,0:T(8,128)S(1)} %bitcast.254, f32[8,128]{1,0:T(8,128)S(1)} %fusion.109, f32[8,128]{1,0:T(8,128)S(1)} %broadcast_multiply_fusion, f32[1152]{0:T(1024)S(1)} %convert_element_type.183, ...), kind=kOutput, calls=%fused_computation.117 | convolution fusion | flops 10163844096 | bytes 28189696 | tf_op jit(solution)/shard_map/itf,df->itd/dot_general | solution.py:192
  710.9 4.4 fusion.71
  715.4 19.1 %fusion.54 = bf16[1152,4304]{1,0:T(8,128)(2,1)} fusion(bf16[8,128,4304]{1,2,0:T(8,128)(2,1)} %get-tuple-element.203, f32[8,128,1152]{2,1,0:T(8,128)} %copy-done.5, f32[1152]{0:T(1024)S(1)} %convert_element_type.184, f32[1152]{0:T(1024)S(1)} %convert_element_type.183, f32[8,128]{1,0:T(8,128)S(1)} %fusion.109, f32[8,128]{1,0:T(8,128)S(1)} %broadcast_multiply_fusion), kind=kOutput, calls=%fused_computation.63 | convolution fusion | flops 10165266432 | bytes 23467008 | tf_op jit(solution)/shard_map/itd,itf->df/dot_general | solution.py:190
  736.3 4.8 convert_bitcast_fusion
  747.3 16.5 fusion.55
  764.1 37.8 %all-to-all-done.2 = bf16[16,8,72,128]{3,2,1,0:T(8,128)(2,1)} async-done(((bf16[16,8,72,128]{3,2,1,0:T(8,128)(2,1)}), bf16[16,8,72,128]{3,2,1,0:T(8,128)(2,1)}, u32[]{:S(2)}, u32[]{:S(2)}) %all-to-all-start.2) | async-done | bytes 2359328 | tf_op jit(solution)/shard_map/all_to_all | solution.py:206
  811.2 220.9 %while.27 = (s32[]{:T(128)}, bf16[16,72,1024]{2,1,0:T(8,128)(2,1)S(1)}, bf16[16,72,1024]{2,1,0:T(8,128)(2,1)}, bf16[16,72,1024]{2,1,0:T(8,128)(2,1)}, bf16[16,72...) while((s32[]{:T(128)}, ...), condition=%wide.region_12.13_spmd, body=%wide.region_10.12_spmd.sunk | while | flops 767778816 | bytes 32969856 | solution.py:208
  1032.1 4.9 copy.108
  1037.0 6.4 copy.109
  1043.4 6.3 copy.110
  1049.7 6.9 pad_maximum_fusion
  1056.7 277.4 %all_to_all.66 = bf16[3,2,8,72,1024]{3,2,1,0,4:T(8,128)(2,1)} all-to-all(bf16[3,2,8,72,1024]{3,2,1,0,4:T(8,128)(2,1)S(1)} %pad_maximum_fusion), channel_id=1, replica_groups=mesh['fsdp'=4,'seq'=8] {'seq'}, dimensions={4} | all-to-all | bytes 14155776 | tf_op jit(solution)/shard_map/all_to_all | solution.py:213
  1334.1 15.4 copy.114
  1349.5 13.9 fusion.63
  1363.4 11.6 copy.115
  1376.8 13.2 copy.133
  1390.1 4.5 convert_reduce_fusion
  1405.6 5.8 fusion.98
  1411.4 8.9 fusion.110
  1424.5 17.1 %all-reduce.16 = (bf16[1152]{0:T(1024)(128)(2,1)S(1)}, bf16[1152]{0:T(1024)(128)(2,1)S(1)}, bf16[1152]{0:T(1024)(128)(2,1)S(1)}, bf16[1152]{0:T(1024)(128)(2,1)S...) all-reduce(bf16[1152]{0:T(1024)(128)(2,1)S(1)} %dynamic-update-slic, ...), channel_id=1, replica_groups=mesh['fsdp'=4,'seq'=8] {'fsdp'}, use_global_device_ids=true, to_apply=%add.6 | all-reduce | flops 12368 | bytes 49472
  1442.2 15.3 reduce-scatter.8.cloned.1.call-done
  1457.5 6.5 add_convert_fusion
  1464.1 19.0 %fusion.94 = bf16[8,128,1152]{2,1,0:T(8,128)(2,1)} fusion(f32[8,128,1152]{2,1,0:T(8,128)} %copy-done.5, bf16[8,128,4304]{1,2,0:T(8,128)(2,1)} %get-tuple-element.198, bf16[4304,1152]{0,1:T(8,128)(2,1)} %all-gather.12.cloned.1.call-done, f32[1152]{0:T(1024)S(1)} %convert_element_type.188), kind=kOutput, calls=%fused_computation.123 | convolution fusion | flops 10157948928 | bytes 25813504 | tf_op jit(solution)/shard_map/itf,fd->itd/dot_general | solution.py:173
  1486.2 29.3 %all-reduce.14 = (bf16[288]{0:T(512)(128)(2,1)S(1)}, bf16[288]{0:T(512)(128)(2,1)S(1)}, bf16[2,288]{1,0:T(2,128)(2,1)S(1)}, bf16[288]{0:T(512)(128)(2,1)S(1)}, b...) all-reduce(bf16[288]{0:T(512)(128)(2,1)S(1)} %dynamic-slice.8, ...), channel_id=1, replica_groups=mesh['fsdp'=4,'seq'=8] {'seq'}, use_global_device_ids=true, to_apply=%region_17.18 | all-reduce | flops 3380 | bytes 13520 | tf_op jit(solution)/shard_map/psum | solution.py:302
  1520.2 130.0 %all-reduce.20.cloned.1.call-done = (bf16[288,3456]{1,0:T(8,128)(2,1)}, bf16[288,1152]{1,0:T(8,128)(2,1)}, bf16[288,4304]{1,0:T(8,128)(2,1)}, bf16[4304,288]{0,1:T(8,128)(2,1)}) async-done(((bf16[288,3456]{1,0:T(8,128)(2,1)}, bf16[288,1152]{1,0:T(8,128)(2,1)}, bf16[288,4304]{1,0:T(8,128)(2,1)}, bf16[4304,288]{0,1:T(8,128)(2,1)}), (bf16[288,3456]{1,0:T(8,128)(2,1)}, bf16[288,1152]{1,0:T(8,128)(2,1)}, ...) | async-done | bytes 7612432 | tf_op jit(solution)/shard_map/psum | solution.py:304
  1650.2 4.5 convert_element_type.213
  (502 shorter events, 471.8 us)
Async XLA Ops:
  7.2 4.2 copy-start.35
  7.2 4.5 copy-start.36
  7.2 4.7 copy-start.37
  7.2 5.0 copy-start.38
  7.2 5.2 copy-start.39
  7.2 5.5 copy-start.32
  7.3 24.2 %copy-start.2 = (bf16[8,128,1152]{2,1,0:T(8,128)(2,1)S(1)}, bf16[8,128,1152]{2,1,0:T(8,128)(2,1)}, u32[]{:S(2)}) copy-start(bf16[8,128,1152]{2,1,0:T(8,128)(2,1)} %param.20) | copy-start | bytes 7077892
  7.3 26.0 %copy-start.34 = (bf16[2,288]{1,0:T(2,128)(2,1)S(1)}, bf16[2,288]{1,0:T(2,128)(2,1)}, u32[]{:S(2)}) copy-start(bf16[2,288]{1,0:T(2,128)(2,1)} %param.25) | copy-start | bytes 3460
  7.3 89.6 %all-gather.6.cloned.1.call-start = ((), (), s32[]{:S(2)}) async-start(), calls=%async_computation.9 | async-start | bytes 9953280 | tf_op jit(solution)/shard_map/all_gather | solution.py:113
  8.0 608.5 %all-gather.8.cloned.1.call-start = ((), (), s32[]{:S(2)}) async-start(), calls=%async_computation.10 | async-start | bytes 3317760 | tf_op jit(solution)/shard_map/all_gather | solution.py:115
  8.8 617.1 %all-gather.10.cloned.1.call-start = ((), (), s32[]{:S(2)}) async-start(), calls=%async_computation.11 | async-start | bytes 12533760 | tf_op jit(solution)/shard_map/all_gather | solution.py:157
  31.5 77.0 %copy-start.15 = (f32[1152]{0:T(1024)}, f32[1152]{0:T(1024)S(1)}, u32[]{:S(2)}) copy-start(f32[1152]{0:T(1024)S(1)} %convert_element_type.178) | copy-start | bytes 13828
  31.5 77.0 %copy-start.28 = (f32[1152]{0:T(1024)}, f32[1152]{0:T(1024)S(1)}, u32[]{:S(2)}) copy-start(f32[1152]{0:T(1024)S(1)} %convert_element_type.179) | copy-start | bytes 13828
  31.9 76.6 %copy-start.17 = (f32[8,128]{1,0:T(8,128)}, f32[8,128]{1,0:T(8,128)S(1)}, u32[]{:S(2)}) copy-start(f32[8,128]{1,0:T(8,128)S(1)} %broadcast_multiply_fusion.1) | copy-start | bytes 12292
  32.7 75.8 %copy-start.21 = (f32[8,128]{1,0:T(8,128)}, f32[8,128]{1,0:T(8,128)S(1)}, u32[]{:S(2)}) copy-start(f32[8,128]{1,0:T(8,128)S(1)} %fusion.108) | copy-start | bytes 12292
  128.3 5.6 copy-start.41
  128.3 160.7 %all-to-all-start = ((bf16[3,16,8,72,128]{4,3,0,2,1:T(8,128)(2,1)}), bf16[3,16,8,72,128]{4,3,0,2,1:T(8,128)(2,1)}, u32[]{:S(2)}, u32[]{:S(2)}) async-start(bf16[3,16,8,72,128]{4,3,0,2,1:T(8,128)(2,1)} %copy.99), calls=%async_computation | async-start | bytes 14155776 | tf_op jit(solution)/shard_map/all_to_all | solution.py:131
  133.2 517.4 %all-gather.12.cloned.1.call-start = ((), (), s32[]{:S(2)}) async-start(), calls=%async_computation.12 | async-start | bytes 12533760 | tf_op jit(solution)/shard_map/all_gather | solution.py:159
  505.4 6.3 copy-start.42
  511.7 98.5 %all-to-all-start.1 = ((bf16[2,8,72,1024]{2,1,0,3:T(8,128)(2,1)}), bf16[2,8,72,1024]{2,1,0,3:T(8,128)(2,1)}, u32[]{:S(2)}, u32[]{:S(2)}) async-start(bf16[2,8,72,1024]{2,1,0,3:T(8,128)(2,1)} %bitcast.255), calls=%async_computation.1 | async-start | bytes 8388608 | tf_op jit(solution)/shard_map/all_to_all | solution.py:141
  516.2 926.0 %reduce-scatter.10.cloned.1.call-start = ((), (), s32[]{:S(2)}) async-start(), calls=%async_computation.14 | async-start | bytes 3317760 | tf_op jit(solution)/shard_map/reduce_scatter | solution.py:263
  625.9 57.3 %slice-start = ((s8[4718592]{0:T(1024)(128)(4,1)}), s8[524288]{0:T(1024)(128)(4,1)S(1)}, s32[]{:S(2)}) async-start(s8[4718592]{0:T(1024)(128)(4,1)} %bitcast.253), calls=%async_computation.19 | async-start | bytes 1048576
  650.7 32.5 %slice-start.1 = ((s8[4718592]{0:T(1024)(128)(4,1)}), s8[4194304]{0:T(1024)(128)(4,1)S(1)}, s32[]{:S(2)}) async-start(s8[4718592]{0:T(1024)(128)(4,1)} %bitcast.253), calls=%async_computation.20 | async-start | bytes 8388608
  707.1 3.8 copy-start.9
  715.4 726.9 %reduce-scatter.12.cloned.1.call-start = ((), (), s32[]{:S(2)}) async-start(), calls=%async_computation.15 | async-start | bytes 12533760 | tf_op jit(solution)/shard_map/reduce_scatter | solution.py:275
  741.1 6.2 copy-start.8
  742.9 59.0 %all-to-all-start.2 = ((bf16[16,8,72,128]{3,2,1,0:T(8,128)(2,1)}), bf16[16,8,72,128]{3,2,1,0:T(8,128)(2,1)}, u32[]{:S(2)}, u32[]{:S(2)}) async-start(bf16[16,8,72,128]{3,2,1,0:T(8,128)(2,1)} %copy.106), calls=%async_computation.2 | async-start | bytes 4718592 | tf_op jit(solution)/shard_map/all_to_all | solution.py:206
  747.2 695.0 %reduce-scatter.14.cloned.1.call-start = ((), (), s32[]{:S(2)}) async-start(), calls=%async_computation.16 | async-start | bytes 12533760 | tf_op jit(solution)/shard_map/reduce_scatter | solution.py:281
  763.8 693.7 %reduce-scatter.8.cloned.1.call-start = ((), (), s32[]{:S(2)}) async-start(), calls=%async_computation.13 | async-start | bytes 9953280 | tf_op jit(solution)/shard_map/reduce_scatter | solution.py:257
  1334.0 15.4 copy-start.3
  1334.0 15.4 copy-start.16
  1334.0 15.4 copy-start.18
  1334.0 15.4 copy-start.22
  1334.0 15.4 copy-start.29
  1334.1 15.4 copy-start.44
  1375.0 110.2 %reduce-scatter.16.cloned.1.call-start = ((), (), s32[]{:S(2)}) async-start(), calls=%async_computation.17 | async-start | bytes 368640
  1390.1 5.6 copy-start.1
  1404.5 6.8 slice-start.2
  1405.6 5.8 slice-start.3
  1411.4 8.9 copy-start.24
  1420.3 4.1 copy-start.25
  1420.3 4.1 copy-start.26
  1420.3 4.1 copy-start.27
  1420.3 4.2 copy-start.30
  1420.3 4.2 copy-start.31
  1420.4 229.8 %all-reduce.20.cloned.1.call-start = ((), (), s32[]{:S(2)}) async-start(), calls=%async_computation.18 | async-start | bytes 15335424 | tf_op jit(solution)/shard_map/psum | solution.py:304
  1424.4 33.1 %copy-start.20 = (f32[8,128]{1,0:T(8,128)S(1)}, f32[8,128]{1,0:T(8,128)}, u32[]{:S(2)}) copy-start(f32[8,128]{1,0:T(8,128)} %copy-done.19) | copy-start | bytes 12292
  1650.2 4.5 copy-start.11
  (29 other events, 62.1 us)
Sparse Core Ops, SparseCore 0:
  9.9 86.9 all-gather.5
  98.8 39.7 all-gather.7
  140.4 101.0 all-gather.9
  243.3 101.0 all-gather.11
  715.5 38.3 reduce-scatter.9
  756.9 99.6 reduce-scatter.11
  859.8 99.6 reduce-scatter.13
  1375.1 82.3 reduce-scatter.7
  1460.8 24.3 reduce-scatter.15
  1487.7 162.3 all-reduce.19
where the time goes:
time: 1680 us; the launch traced here: 1670 us
  waiting for transfers between devices  492 us (29%)
  matrix products  447 us (27%)
  blocking collectives  350 us (21%)
  local copies, waits for them, and re-layouts  242 us (14%)
  other arithmetic  102 us (6%)
  between operations  18 us (1%)
    all_to_all x1, blocking collectives, on_device(): lax.all_to_all(for_sending(grad_stack), 'seq', split_axis=4, concat_axis=...  277 us
    all_to_all x1, waiting for transfers between devices, on_device(): lax.all_to_all(stacked, 'seq', split_axis=1, concat_axis=4, tiled=True)  155 us
    psum x1, waiting for transfers between devices, on_device(): lax.psum(part_qkv.astype(jnp.bfloat16), 'seq').astype(jnp.float32)  130 us
    all_to_all x1, waiting for transfers between devices, on_device(): lax.all_to_all(for_sending(mixed_items.reshape(local_heads, image_count,...  93.5 us
    dot_general x16, matrix products, attend_item(): jnp.einsum('qk,dk->dq', softmax_low, values, preferred_element_type=jnp.f...  64.5 us
    all_gather x1, waiting for transfers between devices, on_device(): lax.all_gather(w_qkv, 'fsdp', axis=0, tiled=True)  55.8 us
    dot_general x16, matrix products, attend_back(): jnp.einsum('qk,dq->dk', softmax_out.astype(jnp.bfloat16), grad_rows, pref...  42.4 us
    all_to_all x1, waiting for transfers between devices, on_device(): lax.all_to_all(grad_mixed, 'seq', split_axis=0, concat_axis=3, tiled=True)  37.8 us
  transfers between devices with their start and end apart: 13, of which 7 were waited for; matrix products, arithmetic and copies ran while one was open for 41% of the time, Pallas kernels for 0%

commit v1 on v0

--- a/solution.py
+++ b/solution.py
@@ -301,7 +301,7 @@
     ) = (
         lax.psum(part_gone.astype(jnp.bfloat16), "seq").astype(jnp.float32),
         lax.psum(part_bone.astype(jnp.bfloat16), "seq").astype(jnp.float32),
-        lax.psum(part_qkv.astype(jnp.bfloat16), "seq").astype(jnp.float32),
+        jnp.sum(lax.all_gather(part_qkv.astype(jnp.bfloat16), "seq"), axis=0).astype(jnp.float32),
         lax.psum(part_qvb.astype(jnp.bfloat16), "seq").astype(jnp.float32),
         lax.psum(part_outw.astype(jnp.bfloat16), "seq").astype(jnp.float32),
         lax.psum(part_outb.astype(jnp.bfloat16), "seq").astype(jnp.float32),

time: 1680 us -> 1790 us (1.065)
  waiting for transfers between devices: 492 us -> 597 us
    all_gather x0 -> x1, waiting for transfers between devices: none -> 137 us  [on_device(): lax.all_gather(part_qkv.astype(jnp.bfloat16), 'seq')]
    psum x1, waiting for transfers between devices: 130 us -> 53.2 us  [on_device(): lax.psum(part_outw.astype(jnp.bfloat16), 'seq').astype(jnp.float32)]
    reduce_scatter x1, waiting for transfers between devices: 15.3 us -> 60.8 us  [on_device(): lax.psum_scatter(grad_qkv.astype(jnp.bfloat16), 'fsdp', scatter_dimension...]
  transfers between devices with their start and end apart: 13 -> 14, of which waited for: 7 -> 7; matrix products, arithmetic and copies ran while one was open for 41% -> 38% of each run, Pallas kernels for 0% -> 0%
where the time goes in v1:
time: 1790 us; the launch traced here: 1780 us
  waiting for transfers between devices  597 us (33%)
  matrix products  447 us (25%)
  blocking collectives  348 us (19%)
  local copies, waits for them, and re-layouts  241 us (13%)
  other arithmetic  110 us (6%)
    all_to_all x1, blocking collectives, on_device(): lax.all_to_all(for_sending(grad_stack), 'seq', split_axis=4, concat_axis=...  278 us
    all_to_all x1, waiting for transfers between devices, on_device(): lax.all_to_all(stacked, 'seq', split_axis=1, concat_axis=4, tiled=True)  155 us
    all_gather x1, waiting for transfers between devices, on_device(): lax.all_gather(part_qkv.astype(jnp.bfloat16), 'seq')  137 us
    all_to_all x1, waiting for transfers between devices, on_device(): lax.all_to_all(for_sending(mixed_items.reshape(local_heads, image_count,...  93.7 us
    dot_general x16, matrix products, attend_item(): jnp.einsum('qk,dk->dq', softmax_low, values, preferred_element_type=jnp.f...  64.5 us
    reduce_scatter x1, waiting for transfers between devices, on_device(): lax.psum_scatter(grad_qkv.astype(jnp.bfloat16), 'fsdp', scatter_dimension...  60.8 us
    all_gather x1, waiting for transfers between devices, on_device(): lax.all_gather(w_qkv, 'fsdp', axis=0, tiled=True)  55.8 us
    psum x1, waiting for transfers between devices, on_device(): lax.psum(part_outw.astype(jnp.bfloat16), 'seq').astype(jnp.float32)  53.2 us
  transfers between devices with their start and end apart: 14, of which 7 were waited for; matrix products, arithmetic and copies ran while one was open for 38% of the time, Pallas kernels for 0%

profile of v1, /device:TPU:0, one launch (start us, length us, event | category | flops | bytes accessed | tf_op | source)
XLA Modules:
  0.0 1776.6 jit_solution(1051532174281180062)
XLA Ops:
  13.0 18.5 %all-reduce.17 = (bf16[1152]{0:T(1024)(128)(2,1)S(1)}, bf16[1152]{0:T(1024)(128)(2,1)S(1)}, bf16[1152]{0:T(1024)(128)(2,1)S(1)}, bf16[1152]{0:T(1024)(128)(2,1)S...) all-reduce(bf16[1152]{0:T(1024)(128)(2,1)S(1)} %dynamic-update-slic, ...), channel_id=1, replica_groups=mesh['fsdp'=4,'seq'=8] {'fsdp'}, use_global_device_ids=true, to_apply=%add.1 | all-reduce | flops 10064 | bytes 40256
  33.3 7.6 all-gather.1
  41.2 55.8 %all-gather.8.cloned.1.call-done = bf16[1152,3456]{1,0:T(8,128)(2,1)} async-done(((bf16[288,3456]{1,0:T(8,128)(2,1)}), bf16[1152,3456]{1,0:T(8,128)(2,1)}) %all-gather.8.cloned.1.call-update) | async-done | bytes 7962640 | tf_op jit(solution)/shard_map/all_gather | solution.py:113
  96.9 11.6 copy.96
  108.5 12.5 convolution_bitcast_fusion.3
  123.5 4.7 copy.98
  128.3 5.0 all-to-all-start
  133.9 155.1 %all-to-all-done = bf16[3,16,8,72,128]{4,3,0,2,1:T(8,128)(2,1)} async-done(((bf16[3,16,8,72,128]{4,3,0,2,1:T(8,128)(2,1)}), bf16[3,16,8,72,128]{4,3,0,2,1:T(8,128)(2,1)}, u32[]{:S(2)}, u32[]{:S(2)}) %all-to-all-start) | async-done | bytes 7077920 | tf_op jit(solution)/shard_map/all_to_all | solution.py:131
  289.0 7.7 fusion.114
  299.6 4.9 reshape_squeeze.10
  304.5 4.6 copy.101
  309.1 4.9 reshape_squeeze.11
  314.1 4.6 copy.99
  318.7 4.9 reshape_squeeze.9
  325.3 180.0 %while.26 = (s32[]{:T(128)}, bf16[16,72,1024]{2,1,0:T(8,128)(2,1)}, f32[16,1024]{1,0:T(8,128)}, bf16[16,72,1024]{2,1,0:T(8,128)(2,1)}, s32[16]{0:T(128)S(1)}, /*...) while((s32[]{:T(128)}, bf16[16,72,1024]{2,1,0:T(8,128)(2,1)}, ...), condition=%wide.region_5.6_spmd, body=%wide.region_2.5_spmd.sunk | while | flops 311500800 | bytes 29997196 | solution.py:138
  505.3 6.3 copy.102
  511.6 4.6 all-to-all-start.1
  516.5 93.7 %all-to-all-done.1 = bf16[2,8,72,1024]{2,1,0,3:T(8,128)(2,1)} async-done(((bf16[2,8,72,1024]{2,1,0,3:T(8,128)(2,1)}), bf16[2,8,72,1024]{2,1,0,3:T(8,128)(2,1)}, u32[]{:S(2)}, u32[]{:S(2)}) %all-to-all-start.1) | async-done | bytes 2359328 | tf_op jit(solution)/shard_map/all_to_all | solution.py:141
  610.2 6.3 copy.104
  616.5 6.5 fusion.116
  625.9 24.8 %multiply_convert_fusion.1 = (bf16[8,128,4304]{1,2,0:T(8,128)(2,1)}, f32[8,128,4304]{1,2,0:T(8,128)}) fusion(f32[4304]{0:T(1024)S(1)} %convert_element_type.188, bf16[1152,4304]{1,0:T(8,128)(2,1)} %all-gather.12.cloned.1.call-done, f32[8,128,1152]{2,1,0:T(8,128)} %copy-done.4, f32[1152]{0:T(1024)S(1)} %convert_element_type.186, ...), kind=kOutput, calls=%fused_computation.72 | convolution fusion | flops 10204381184 | bytes 41113408 | tf_op jit(solution)/shard_map/itd,df->itf/dot_general | solution.py:166
  650.7 32.5 %fusion.117 = (bf16[4304]{0:T(1024)(128)(2,1)}, bf16[8,128,4304]{1,2,0:T(8,128)(2,1)}) fusion(f32[8,128,4304]{1,2,0:T(8,128)} %get-tuple-element.198, f32[4304]{0:T(1024)S(1)} %convert_element_type.188, bf16[8,128,1152]{2,1,0:T(8,128)(2,1)} %param.34, bf16[4304,1152]{0,1:T(8,128)(2,1)} %all-gather.14.cloned.1.call-done), kind=kOutput, calls=%fused_computation.155 | convolution fusion | flops 10251366400 | bytes 38745312 | tf_op jit(solution)/shard_map/itd,fd->itf/dot_general | solution.py:187
  683.2 20.8 %multiply_reduce_fusion.1 = (bf16[1152]{0:T(1024)(128)(2,1)}, f32[8,128]{1,0:T(8,128)S(1)}, bf16[1152]{0:T(1024)(128)(2,1)}, f32[8,128,1152]{2,1,0:T(8,128)}) fusion(f32[8,128,1152]{2,1,0:T(8,128)S(1)} %bitcast.255, f32[8,128]{1,0:T(8,128)S(1)} %fusion.109, f32[8,128]{1,0:T(8,128)S(1)} %broadcast_multiply_fusion, f32[1152]{0:T(1024)S(1)} %convert_element_type.185, ...), kind=kOutput, calls=%fused_computation.117 | convolution fusion | flops 10163844096 | bytes 28189696 | tf_op jit(solution)/shard_map/itf,df->itd/dot_general | solution.py:192
  715.7 18.9 %fusion.54 = bf16[1152,4304]{1,0:T(8,128)(2,1)} fusion(bf16[8,128,4304]{1,2,0:T(8,128)(2,1)} %get-tuple-element.202, f32[8,128,1152]{2,1,0:T(8,128)} %copy-done.4, f32[1152]{0:T(1024)S(1)} %convert_element_type.186, f32[1152]{0:T(1024)S(1)} %convert_element_type.185, f32[8,128]{1,0:T(8,128)S(1)} %fusion.109, f32[8,128]{1,0:T(8,128)S(1)} %broadcast_multiply_fusion), kind=kOutput, calls=%fused_computation.63 | convolution fusion | flops 10165266432 | bytes 23467008 | tf_op jit(solution)/shard_map/itd,itf->df/dot_general | solution.py:190
  736.4 4.8 convert_bitcast_fusion
  747.4 16.3 fusion.55
  764.0 38.0 %all-to-all-done.2 = bf16[16,8,72,128]{3,2,1,0:T(8,128)(2,1)} async-done(((bf16[16,8,72,128]{3,2,1,0:T(8,128)(2,1)}), bf16[16,8,72,128]{3,2,1,0:T(8,128)(2,1)}, u32[]{:S(2)}, u32[]{:S(2)}) %all-to-all-start.2) | async-done | bytes 2359328 | tf_op jit(solution)/shard_map/all_to_all | solution.py:206
  811.4 220.9 %while.27 = (s32[]{:T(128)}, bf16[16,72,1024]{2,1,0:T(8,128)(2,1)S(1)}, bf16[16,72,1024]{2,1,0:T(8,128)(2,1)}, bf16[16,72,1024]{2,1,0:T(8,128)(2,1)}, bf16[16,72...) while((s32[]{:T(128)}, ...), condition=%wide.region_12.13_spmd, body=%wide.region_10.12_spmd.sunk | while | flops 767778816 | bytes 32969856 | solution.py:208
  1032.2 4.9 copy.107
  1037.1 6.4 copy.108
  1043.5 6.3 copy.109
  1049.8 6.9 pad_maximum_fusion
  1056.8 278.2 %all_to_all.66 = bf16[3,2,8,72,1024]{3,2,1,0,4:T(8,128)(2,1)} all-to-all(bf16[3,2,8,72,1024]{3,2,1,0,4:T(8,128)(2,1)S(1)} %pad_maximum_fusion), channel_id=1, replica_groups=mesh['fsdp'=4,'seq'=8] {'seq'}, dimensions={4} | all-to-all | bytes 14155776 | tf_op jit(solution)/shard_map/all_to_all | solution.py:213
  1335.0 15.3 copy.113
  1350.4 13.9 fusion.63
  1364.3 11.5 copy.114
  1375.9 13.5 copy.132
  1396.3 60.8 %reduce-scatter.8.cloned.1.call-done = bf16[288,3456]{1,0:T(8,128)(2,1)} async-done(((bf16[1152,3456]{1,0:T(8,128)(2,1)}), bf16[288,3456]{1,0:T(8,128)(2,1)}) %reduce-scatter.8.cloned.1.call-update) | async-done | bytes 1990672 | tf_op jit(solution)/shard_map/reduce_scatter | solution.py:257
  1465.6 5.2 fusion.98
  1470.8 9.2 fusion.110
  1484.4 16.0 all-reduce.16
  1501.0 6.7 add_convert_fusion
  1507.7 19.1 %fusion.94 = bf16[8,128,1152]{2,1,0:T(8,128)(2,1)} fusion(f32[8,128,1152]{2,1,0:T(8,128)} %copy-done.4, bf16[8,128,4304]{1,2,0:T(8,128)(2,1)} %get-tuple-element.197, bf16[4304,1152]{0,1:T(8,128)(2,1)} %all-gather.14.cloned.1.call-done, f32[1152]{0:T(1024)S(1)} %convert_element_type.190), kind=kOutput, calls=%fused_computation.123 | convolution fusion | flops 10157948928 | bytes 25813504 | tf_op jit(solution)/shard_map/itf,fd->itd/dot_general | solution.py:173
  1527.7 27.2 %all-reduce.14 = (bf16[288]{0:T(512)(128)(2,1)S(1)}, bf16[288]{0:T(512)(128)(2,1)S(1)}, bf16[2,288]{1,0:T(2,128)(2,1)S(1)}, bf16[288]{0:T(512)(128)(2,1)S(1)}, b...) all-reduce(bf16[288]{0:T(512)(128)(2,1)S(1)} %dynamic-slice.8, ...), channel_id=1, replica_groups=mesh['fsdp'=4,'seq'=8] {'seq'}, use_global_device_ids=true, to_apply=%region_17.18 | all-reduce | flops 3380 | bytes 13520 | tf_op jit(solution)/shard_map/psum | solution.py:302
  1559.6 53.2 %all-reduce.20.cloned.1.call-done = (bf16[288,1152]{1,0:T(8,128)(2,1)}, bf16[288,4304]{1,0:T(8,128)(2,1)}, bf16[4304,288]{0,1:T(8,128)(2,1)}) async-done(((bf16[288,1152]{1,0:T(8,128)(2,1)}, bf16[288,4304]{1,0:T(8,128)(2,1)}, bf16[4304,288]{0,1:T(8,128)(2,1)}), (bf16[288,1152]{1,0:T(8,128)(2,1)}, bf16[288,4304]{1,0:T(8,128)(2,1)}, bf16[4304,288]{0,1:T(8,128)(2,1)})) %all-reduce.20.cloned.1.call-update) | async-done | bytes 5621776 | tf_op jit(solution)/shard_map/psum | solution.py:306
  1612.8 4.5 convert_element_type.215
  1621.0 137.5 %all-gather.16.cloned.1.call-done = bf16[2304,3456]{1,0:T(8,128)(2,1)} async-done(((bf16[288,3456]{1,0:T(8,128)(2,1)}), bf16[2304,3456]{1,0:T(8,128)(2,1)}) %all-gather.16.cloned.1.call-update) | async-done | bytes 15925264 | tf_op jit(solution)/shard_map/all_gather | solution.py:304
  1758.5 9.1 reduce_sum.225
  (502 shorter events, 476.7 us)
Async XLA Ops:
  7.2 4.2 copy-start.33
  7.2 4.5 copy-start.34
  7.2 4.7 copy-start.35
  7.2 5.0 copy-start.36
  7.2 5.2 copy-start.37
  7.2 5.5 copy-start.30
  7.3 24.2 %copy-start.1 = (bf16[8,128,1152]{2,1,0:T(8,128)(2,1)S(1)}, bf16[8,128,1152]{2,1,0:T(8,128)(2,1)}, u32[]{:S(2)}) copy-start(bf16[8,128,1152]{2,1,0:T(8,128)(2,1)} %param.20) | copy-start | bytes 7077892
  7.3 26.0 %copy-start.32 = (bf16[2,288]{1,0:T(2,128)(2,1)S(1)}, bf16[2,288]{1,0:T(2,128)(2,1)}, u32[]{:S(2)}) copy-start(bf16[2,288]{1,0:T(2,128)(2,1)} %param.25) | copy-start | bytes 3460
  7.3 89.6 %all-gather.8.cloned.1.call-start = ((), (), s32[]{:S(2)}) async-start(), calls=%async_computation.9 | async-start | bytes 9953280 | tf_op jit(solution)/shard_map/all_gather | solution.py:113
  8.0 608.5 %all-gather.10.cloned.1.call-start = ((), (), s32[]{:S(2)}) async-start(), calls=%async_computation.10 | async-start | bytes 3317760 | tf_op jit(solution)/shard_map/all_gather | solution.py:115
  8.8 617.1 %all-gather.12.cloned.1.call-start = ((), (), s32[]{:S(2)}) async-start(), calls=%async_computation.11 | async-start | bytes 12533760 | tf_op jit(solution)/shard_map/all_gather | solution.py:157
  31.5 77.0 %copy-start.13 = (f32[1152]{0:T(1024)}, f32[1152]{0:T(1024)S(1)}, u32[]{:S(2)}) copy-start(f32[1152]{0:T(1024)S(1)} %convert_element_type.180) | copy-start | bytes 13828
  31.5 77.0 %copy-start.26 = (f32[1152]{0:T(1024)}, f32[1152]{0:T(1024)S(1)}, u32[]{:S(2)}) copy-start(f32[1152]{0:T(1024)S(1)} %convert_element_type.181) | copy-start | bytes 13828
  31.9 76.6 %copy-start.15 = (f32[8,128]{1,0:T(8,128)}, f32[8,128]{1,0:T(8,128)S(1)}, u32[]{:S(2)}) copy-start(f32[8,128]{1,0:T(8,128)S(1)} %broadcast_multiply_fusion.1) | copy-start | bytes 12292
  32.7 75.8 %copy-start.19 = (f32[8,128]{1,0:T(8,128)}, f32[8,128]{1,0:T(8,128)S(1)}, u32[]{:S(2)}) copy-start(f32[8,128]{1,0:T(8,128)S(1)} %fusion.108) | copy-start | bytes 12292
  128.3 5.6 copy-start.39
  128.3 160.7 %all-to-all-start = ((bf16[3,16,8,72,128]{4,3,0,2,1:T(8,128)(2,1)}), bf16[3,16,8,72,128]{4,3,0,2,1:T(8,128)(2,1)}, u32[]{:S(2)}, u32[]{:S(2)}) async-start(bf16[3,16,8,72,128]{4,3,0,2,1:T(8,128)(2,1)} %copy.98), calls=%async_computation | async-start | bytes 14155776 | tf_op jit(solution)/shard_map/all_to_all | solution.py:131
  133.2 517.5 %all-gather.14.cloned.1.call-start = ((), (), s32[]{:S(2)}) async-start(), calls=%async_computation.12 | async-start | bytes 12533760 | tf_op jit(solution)/shard_map/all_gather | solution.py:159
  505.3 6.3 copy-start.40
  511.6 98.5 %all-to-all-start.1 = ((bf16[2,8,72,1024]{2,1,0,3:T(8,128)(2,1)}), bf16[2,8,72,1024]{2,1,0,3:T(8,128)(2,1)}, u32[]{:S(2)}, u32[]{:S(2)}) async-start(bf16[2,8,72,1024]{2,1,0,3:T(8,128)(2,1)} %bitcast.256), calls=%async_computation.1 | async-start | bytes 8388608 | tf_op jit(solution)/shard_map/all_to_all | solution.py:141
  516.2 879.1 %reduce-scatter.10.cloned.1.call-start = ((), (), s32[]{:S(2)}) async-start(), calls=%async_computation.14 | async-start | bytes 3317760 | tf_op jit(solution)/shard_map/reduce_scatter | solution.py:263
  625.9 57.4 %slice-start = ((s8[4718592]{0:T(1024)(128)(4,1)}), s8[524288]{0:T(1024)(128)(4,1)S(1)}, s32[]{:S(2)}) async-start(s8[4718592]{0:T(1024)(128)(4,1)} %bitcast.254), calls=%async_computation.20 | async-start | bytes 1048576
  650.7 32.6 %slice-start.1 = ((s8[4718592]{0:T(1024)(128)(4,1)}), s8[4194304]{0:T(1024)(128)(4,1)S(1)}, s32[]{:S(2)}) async-start(s8[4718592]{0:T(1024)(128)(4,1)} %bitcast.254), calls=%async_computation.21 | async-start | bytes 8388608
  707.4 3.8 copy-start.8
  715.6 679.7 %reduce-scatter.12.cloned.1.call-start = ((), (), s32[]{:S(2)}) async-start(), calls=%async_computation.15 | async-start | bytes 12533760 | tf_op jit(solution)/shard_map/reduce_scatter | solution.py:275
  741.2 6.2 copy-start.7
  742.9 59.0 %all-to-all-start.2 = ((bf16[16,8,72,128]{3,2,1,0:T(8,128)(2,1)}), bf16[16,8,72,128]{3,2,1,0:T(8,128)(2,1)}, u32[]{:S(2)}, u32[]{:S(2)}) async-start(bf16[16,8,72,128]{3,2,1,0:T(8,128)(2,1)} %copy.105), calls=%async_computation.2 | async-start | bytes 4718592 | tf_op jit(solution)/shard_map/all_to_all | solution.py:206
  747.3 648.0 %reduce-scatter.14.cloned.1.call-start = ((), (), s32[]{:S(2)}) async-start(), calls=%async_computation.16 | async-start | bytes 12533760 | tf_op jit(solution)/shard_map/reduce_scatter | solution.py:281
  763.8 693.3 %reduce-scatter.8.cloned.1.call-start = ((), (), s32[]{:S(2)}) async-start(), calls=%async_computation.13 | async-start | bytes 9953280 | tf_op jit(solution)/shard_map/reduce_scatter | solution.py:257
  1335.0 15.4 copy-start.2
  1335.0 15.4 copy-start.14
  1335.0 15.4 copy-start.16
  1335.0 15.4 copy-start.20
  1335.0 15.4 copy-start.27
  1335.0 15.4 copy-start.42
  1375.9 150.9 %reduce-scatter.16.cloned.1.call-start = ((), (), s32[]{:S(2)}) async-start(), calls=%async_computation.18 | async-start | bytes 368640
  1393.8 64.6 %copy-start.38 = (bf16[288]{0:T(512)(128)(2,1)S(1)}, bf16[288]{0:T(512)(128)(2,1)}, u32[]{:S(2)}) copy-start(bf16[288]{0:T(512)(128)(2,1)} %param.33) | copy-start | bytes 1732
  1395.2 217.6 %all-reduce.20.cloned.1.call-start = ((), (), s32[]{:S(2)}) async-start(), calls=%async_computation.19 | async-start | bytes 11354112 | tf_op jit(solution)/shard_map/psum | solution.py:306
  1395.8 362.7 %all-gather.16.cloned.1.call-start = ((), (), s32[]{:S(2)}) async-start(), calls=%async_computation.17 | async-start | bytes 17915904 | tf_op jit(solution)/shard_map/all_gather | solution.py:304
  1460.5 4.2 slice-start.2
  1470.8 9.3 copy-start.22
  1480.0 4.3 copy-start.23
  1480.0 4.3 copy-start.24
  1480.1 4.3 copy-start.25
  1480.1 4.3 copy-start.28
  1480.1 4.3 copy-start.29
  1480.1 20.9 %copy-start.18 = (f32[8,128]{1,0:T(8,128)S(1)}, f32[8,128]{1,0:T(8,128)}, u32[]{:S(2)}) copy-start(f32[8,128]{1,0:T(8,128)} %copy-done.17) | copy-start | bytes 12292
  1612.8 4.5 copy-start.10
  (28 other events, 59.5 us)
Sparse Core Ops, SparseCore 0:
  9.9 86.9 all-gather.7
  98.8 39.7 all-gather.9
  140.4 101.0 all-gather.11
  243.3 101.0 all-gather.13
  715.8 38.3 reduce-scatter.9
  757.2 99.7 reduce-scatter.11
  860.2 99.7 reduce-scatter.13
  1376.0 81.0 reduce-scatter.7
  1460.5 24.4 reduce-scatter.15
  1487.4 125.3 all-reduce.19
  1614.4 144.0 all-gather.15
